TPU v7x, 32 devices: a whole 2x2x4 slice. The times are simulated.
32 devices in a mesh: dof: 8 (over y, x, core), tm: 4 (over z).
Axes of the slice: x: 2, y: 2, z: 4, core: 2. Of those that a mesh axis runs over, the one named last changes fastest.
Arguments:
- snapshots: bfloat16 [163840, 1024], P('dof', 'tm'), may hold values from -6 to 6
- basis: bfloat16 [163840, 64], P('dof'), may hold values from -0.015625 to 0.015625
Outputs:
- gram: float32 [2144, 2144], P('tm', 'dof')
- coords: float32 [64, 1024], P(None, 'tm')
All inputs are finite; a program needn't handle non-finite values.
Results may differ from a plain program's by a relative error of at most 0.0021.
Values may be sent and summed in bfloat16 or wider, within the bound.
No kernel may reach another device: no remote copies, remote signals or barrier semaphores. Data moves between devices by JAX's collectives and lax.ppermute only.
A program may use at most 64 MiB of HBM per device.

v0:
```python
import jax
import jax.numpy as jnp
import numpy as np
from jax import lax
from jax.sharding import PartitionSpec as P


def build_features(coords):
    modes = coords.shape[0]
    upper_i, upper_j = np.triu_indices(modes)
    quad = coords[upper_i, :] * coords[upper_j, :]
    return jnp.concatenate([coords, quad], axis=0).astype(jnp.bfloat16)


def on_device(snapshots, basis):
    partial_proj = lax.dot_general(
        basis, snapshots, (((0,), (0,)), ((), ())), preferred_element_type=jnp.float32
    )
    coords = lax.psum(partial_proj, "dof")
    features = build_features(coords)
    feature_count = features.shape[0]
    inverse_total = 1.0 / (features.shape[1] * lax.axis_size("tm"))
    owned_rows = feature_count // lax.axis_size("tm")
    col_width = feature_count // lax.axis_size("dof")
    col_start = lax.axis_index("dof") * col_width
    row_start = lax.axis_index("tm") * owned_rows
    initial = jnp.zeros((owned_rows, col_width), jnp.float32)
    piece = lax.all_gather(features, "tm", axis=1, tiled=True)
    row_part = lax.dynamic_slice_in_dim(piece, row_start, owned_rows, 0)
    col_part = lax.dynamic_slice_in_dim(piece, col_start, col_width, 0)
    product = lax.dot_general(
        row_part, col_part, (((1,), (1,)), ((), ())), preferred_element_type=jnp.float32
    )
    gram = initial + product * inverse_total
    return (gram, coords)


def solution(mesh):
    placed = (P("dof", "tm"), P("dof", None))
    return jax.shard_map(
        on_device,
        mesh=mesh,
        in_specs=placed,
        out_specs=(P("tm", "dof"), P(None, "tm")),
        check_vma=False,
    )
```

profile of v0, /device:TPU:0, one launch (start us, length us, event | category | flops | bytes accessed | tf_op | source)
XLA Modules:
  0.0 182.3 jit_solution(5816619657642350401)
XLA Ops:
  7.2 0.0 copy-start
  7.2 0.0 copy-start.2
  7.2 0.0 copy-start.3
  7.2 0.0 all-reduce.2.cloned.1.call-start
  7.2 1.7 copy-done
  8.9 6.4 %fusion.3 = f32[64,256]{1,0:T(8,128)} fusion(bf16[20480,64]{0,1:T(8,128)(2,1)S(1)} %copy-done, bf16[20480,256]{1,0:T(8,128)(2,1)} %param.6), kind=kOutput, calls=%fused_computation.10 | convolution fusion | flops 671088640 | bytes 13172736 | tf_op jit(solution)/shard_map/dot_general | solution.py:16
  15.3 0.0 all-reduce.2.cloned.1.call-update
  15.4 0.0 all-gather.2.cloned.1.call-start
  15.4 0.0 copy-done.2
  15.4 0.0 copy-done.3
  15.4 56.0 %all-reduce.2.cloned.1.call-done = f32[64,256]{1,0:T(8,128)} async-done(((f32[64,256]{1,0:T(8,128)}), f32[64,256]{1,0:T(8,128)}) %all-reduce.2.cloned.1.call-update) | async-done | bytes 65552 | tf_op jit(solution)/shard_map/psum | solution.py:19
  71.4 0.0 copy-start.1
  71.4 7.3 %gather_fusion = f32[2080,256]{1,0:T(8,128)} fusion(f32[64,256]{1,0:T(8,128)} %all-reduce.2.cloned.1.call-done, s32[3072]{0:T(1024)S(1)} %pad_clamp_fusion.1), kind=kCustom, calls=%fused_computation | custom fusion | bytes 4268160 | tf_op jit(solution)/shard_map/gather | solution.py:11
  78.7 0.0 copy-done.1
  78.7 6.4 %gather_fusion.1 = f32[2080,256]{1,0:T(8,128)} fusion(f32[64,256]{1,0:T(8,128)S(1)} %copy-done.1, s32[3072]{0:T(1024)S(1)} %pad_clamp_fusion), kind=kCustom, calls=%fused_computation.1 | custom fusion | bytes 4268160 | tf_op jit(solution)/shard_map/gather | solution.py:11
  85.0 2.5 %multiply_convert_fusion = bf16[2080,256]{1,0:T(8,128)(2,1)S(1)} fusion(f32[2080,256]{1,0:T(8,128)} %gather_fusion, f32[2080,256]{1,0:T(8,128)} %gather_fusion.1), kind=kLoop, calls=%fused_computation.2 | loop fusion | flops 1064960 | bytes 5324800 | tf_op jit(solution)/shard_map/convert.1
  87.5 1.1 pad_maximum_fusion
  88.6 0.0 all-gather.2.cloned.1.call-update
  88.6 83.3 %all-gather.2.cloned.1.call-done = bf16[2144,1024]{1,0:T(8,128)(2,1)} async-done(((bf16[2144,256]{1,0:T(8,128)(2,1)}), bf16[2144,1024]{1,0:T(8,128)(2,1)}) %all-gather.2.cloned.1.call-update) | async-done | bytes 4390928 | tf_op jit(solution)/shard_map/all_gather | solution.py:28
  171.9 2.9 %convolution_multiply_fusion = f32[536,268]{0,1:T(8,128)} fusion(bf16[2144,1024]{1,0:T(8,128)(2,1)} %all-gather.2.cloned.1.call-done, s32[]{:T(128)S(6)} %select_n.14, s32[]{:T(128)S(6)} %select_n.15), kind=kOutput, calls=%fused_computation.3 | convolution fusion | flops 294334752 | bytes 2229384 | tf_op jit(solution)/shard_map/dot_general | solution.py:31
  174.8 0.6 copy.9
  (3 shorter events, 0.0 us)
Async XLA Ops:
  7.2 1.7 copy-start
  7.2 8.2 %copy-start.2 = (s32[2080]{0:T(1024)S(1)}, s32[2080]{0:T(1024)}, u32[]{:S(2)}) copy-start(s32[2080]{0:T(1024)} %constant.32) | copy-start | bytes 24964
  7.2 8.2 %copy-start.3 = (s32[2080]{0:T(1024)S(1)}, s32[2080]{0:T(1024)}, u32[]{:S(2)}) copy-start(s32[2080]{0:T(1024)} %constant.33) | copy-start | bytes 24964
  7.2 64.2 %all-reduce.2.cloned.1.call-start = ((), (), s32[]{:S(2)}) async-start(), calls=%async_computation | async-start | bytes 131072 | tf_op jit(solution)/shard_map/psum | solution.py:19
  15.4 156.6 %all-gather.2.cloned.1.call-start = ((), (), s32[]{:S(2)}) async-start(), calls=%async_computation.1 | async-start | bytes 5488640 | tf_op jit(solution)/shard_map/all_gather | solution.py:28
  71.4 7.3 %copy-start.1 = (f32[64,256]{1,0:T(8,128)S(1)}, f32[64,256]{1,0:T(8,128)}, u32[]{:S(2)}) copy-start(f32[64,256]{1,0:T(8,128)} %all-reduce.2.cloned.1.call-done) | copy-start | bytes 196612
Sparse Core Ops, SparseCore 0:
  15.5 55.8 all-reduce.1
  88.7 83.1 all-gather.1
where the time goes:
time: 183 us; the launch traced here: 182 us
  waiting for transfers between devices  139 us (76%)
  local copies, waits for them, and re-layouts  15.9 us (9%)
  between operations  14.1 us (8%)
  matrix products  9.32 us (5%)
  other arithmetic  3.55 us (2%)
    all_gather x1, waiting for transfers between devices, on_device(): piece = lax.all_gather(features, 'tm', axis=1, tiled=True)  83.3 us
    psum x1, waiting for transfers between devices, on_device(): coords = lax.psum(partial_proj, 'dof')  56 us
    gather x2, local copies, waits for them, and re-layouts, build_features(): quad = coords[upper_i, :] * coords[upper_j, :]  13.6 us
    dot_general x1, matrix products, on_device(): lax.dot_general(basis, snapshots, (((0,), (0,)), ((), ())), preferred_ele...  6.42 us
  transfers between devices with their start and end apart: 2, of which 2 were waited for; matrix products, arithmetic and copies ran while one was open for 0% of the time, Pallas kernels for 0%

commit v1 on v0

--- a/solution.py
+++ b/solution.py
@@ -25,7 +25,12 @@
     col_start = lax.axis_index("dof") * col_width
     row_start = lax.axis_index("tm") * owned_rows
     initial = jnp.zeros((owned_rows, col_width), jnp.float32)
-    piece = lax.all_gather(features, "tm", axis=1, tiled=True)
+
+    def _follow_outputs(panel):
+        part_now = jnp.concatenate(jax.lax.all_gather(panel, "tm"), 1)
+        return part_now
+
+    piece = _follow_outputs(features)
     row_part = lax.dynamic_slice_in_dim(piece, row_start, owned_rows, 0)
     col_part = lax.dynamic_slice_in_dim(piece, col_start, col_width, 0)
     product = lax.dot_general(

time: 183 us -> 190 us (1.038)
  local copies, waits for them, and re-layouts: 15.9 us -> 22.4 us
    reshape x0 -> x1, local copies, waits for them, and re-layouts: none -> 6.44 us  [_follow_outputs(): part_now = jnp.concatenate(jax.lax.all_gather(panel, 'tm'), 1)]
    another operation x2 -> x0, other arithmetic: 2.46 us -> none
    concatenate x1 -> x3, other arithmetic: 1.08 us -> 3.53 us  [build_features(): return jnp.concatenate([coords, quad], axis=0).astype(jnp.bfloat16)]
where the time goes in v1:
time: 190 us
  waiting for transfers between devices  140 us (74%)
  local copies, waits for them, and re-layouts  22.4 us (12%)
  between operations  14.1 us (7%)
  matrix products  10.4 us (5%)
  other arithmetic  3.54 us (2%)
    all_gather x1, waiting for transfers between devices, _follow_outputs(): part_now = jnp.concatenate(jax.lax.all_gather(panel, 'tm'), 1)  83.5 us
    psum x1, waiting for transfers between devices, on_device(): coords = lax.psum(partial_proj, 'dof')  55.9 us
    gather x2, local copies, waits for them, and re-layouts, build_features(): quad = coords[upper_i, :] * coords[upper_j, :]  13.6 us
    reshape x1, local copies, waits for them, and re-layouts, _follow_outputs(): part_now = jnp.concatenate(jax.lax.all_gather(panel, 'tm'), 1)  6.44 us
    dot_general x1, matrix products, on_device(): lax.dot_general(basis, snapshots, (((0,), (0,)), ((), ())), preferred_ele...  6.44 us
    dot_general x1, matrix products, on_device(): lax.dot_general(row_part, col_part, (((1,), (1,)), ((), ())), preferred_e...  3.95 us
  transfers between devices with their start and end apart: 2, of which 2 were waited for; matrix products, arithmetic and copies ran while one was open for 0% of the time, Pallas kernels for 0%

profile of v1, /device:TPU:0, one launch (start us, length us, event | category | flops | bytes accessed | tf_op | source)
XLA Modules:
  0.0 190.0 jit_solution(8497530983714208273)
XLA Ops:
  7.2 0.0 copy-start
  7.2 0.0 copy-start.2
  7.2 0.0 copy-start.3
  7.2 0.0 all-reduce.2.cloned.1.call-start
  7.2 1.7 copy-done
  8.9 6.4 %fusion.8 = f32[64,256]{1,0:T(8,128)} fusion(bf16[20480,64]{0,1:T(8,128)(2,1)S(1)} %copy-done, bf16[20480,256]{1,0:T(8,128)(2,1)} %param.6), kind=kOutput, calls=%fused_computation.13 | convolution fusion | flops 671088640 | bytes 13172736 | tf_op jit(solution)/shard_map/dot_general | solution.py:16
  15.3 0.0 all-reduce.2.cloned.1.call-update
  15.4 0.0 all-gather.2.cloned.1.call-start
  15.4 0.0 copy-done.2
  15.4 0.0 copy-done.3
  15.5 55.9 %all-reduce.2.cloned.1.call-done = f32[64,256]{1,0:T(8,128)} async-done(((f32[64,256]{1,0:T(8,128)}), f32[64,256]{1,0:T(8,128)}) %all-reduce.2.cloned.1.call-update) | async-done | bytes 65552 | tf_op jit(solution)/shard_map/psum | solution.py:19
  71.4 0.0 copy-start.1
  71.4 7.3 %gather_fusion = f32[2080,256]{1,0:T(8,128)} fusion(f32[64,256]{1,0:T(8,128)} %all-reduce.2.cloned.1.call-done, s32[3072]{0:T(1024)S(1)} %pad_clamp_fusion.1), kind=kCustom, calls=%fused_computation | custom fusion | bytes 4268160 | tf_op jit(solution)/shard_map/gather | solution.py:11
  78.7 0.0 copy-done.1
  78.7 6.4 %gather_fusion.1 = f32[2080,256]{1,0:T(8,128)} fusion(f32[64,256]{1,0:T(8,128)S(1)} %copy-done.1, s32[3072]{0:T(1024)S(1)} %pad_clamp_fusion), kind=kCustom, calls=%fused_computation.1 | custom fusion | bytes 4268160 | tf_op jit(solution)/shard_map/gather | solution.py:11
  85.0 2.5 %fusion.5 = bf16[1,2080,256]{2,1,0:T(8,128)(2,1)S(1)} fusion(f32[2080,256]{1,0:T(8,128)} %gather_fusion, f32[2080,256]{1,0:T(8,128)} %gather_fusion.1), kind=kLoop, calls=%fused_computation.7 | loop fusion | flops 1064960 | bytes 5324800 | tf_op jit(solution)/shard_map/concatenate | solution.py:12
  87.5 1.1 pad_maximum_fusion
  88.6 0.0 all-gather.2.cloned.1.call-update
  88.6 83.5 %all-gather.2.cloned.1.call-done = bf16[4,2144,256]{2,1,0:T(8,128)(2,1)} async-done(((bf16[1,2144,256]{2,1,0:T(8,128)(2,1)}), bf16[4,2144,256]{2,1,0:T(8,128)(2,1)}) %all-gather.2.cloned.1.call-update) | async-done | bytes 4390928 | tf_op jit(solution)/shard_map/all_gather | solution.py:30
  172.1 6.4 %copy.9 = bf16[2144,4,256]{0,2,1:T(8,128)(2,1)} copy(bf16[2144,4,256]{2,0,1:T(8,128)(2,1)} %bitcast.9) | data formatting | bytes 8781824 | tf_op jit(solution)/shard_map/reshape | solution.py:30
  178.6 3.9 %fusion.2 = f32[536,268]{0,1:T(8,128)} fusion(bf16[2144,1024]{0,1:T(8,128)(2,1)} %bitcast.8, s32[]{:T(128)S(6)} %select_n.14, s32[]{:T(128)S(6)} %select_n.15), kind=kOutput, calls=%fused_computation.5 | convolution fusion | flops 294334752 | bytes 2671752 | tf_op jit(solution)/shard_map/dot_general | solution.py:36
  182.5 0.6 copy.11
  (3 shorter events, 0.0 us)
Async XLA Ops:
  7.2 1.7 copy-start
  7.2 8.2 %copy-start.2 = (s32[2080]{0:T(1024)S(1)}, s32[2080]{0:T(1024)}, u32[]{:S(2)}) copy-start(s32[2080]{0:T(1024)} %constant.32) | copy-start | bytes 24964
  7.2 8.3 %copy-start.3 = (s32[2080]{0:T(1024)S(1)}, s32[2080]{0:T(1024)}, u32[]{:S(2)}) copy-start(s32[2080]{0:T(1024)} %constant.33) | copy-start | bytes 24964
  7.2 64.2 %all-reduce.2.cloned.1.call-start = ((), (), s32[]{:S(2)}) async-start(), calls=%async_computation | async-start | bytes 131072 | tf_op jit(solution)/shard_map/psum | solution.py:19
  15.4 156.8 %all-gather.2.cloned.1.call-start = ((), (), s32[]{:S(2)}) async-start(), calls=%async_computation.1 | async-start | bytes 5488640 | tf_op jit(solution)/shard_map/all_gather | solution.py:30
  71.4 7.3 %copy-start.1 = (f32[64,256]{1,0:T(8,128)S(1)}, f32[64,256]{1,0:T(8,128)}, u32[]{:S(2)}) copy-start(f32[64,256]{1,0:T(8,128)} %all-reduce.2.cloned.1.call-done) | copy-start | bytes 196612
Sparse Core Ops, SparseCore 0:
  15.5 55.8 all-reduce.1
  88.7 83.3 all-gather.1

commit v2 on v0

--- a/solution.py
+++ b/solution.py
@@ -16,7 +16,8 @@
     partial_proj = lax.dot_general(
         basis, snapshots, (((0,), (0,)), ((), ())), preferred_element_type=jnp.float32
     )
-    coords = lax.psum(partial_proj, "dof")
+    blocks = lax.all_gather(partial_proj, "dof")
+    coords = jnp.sum(blocks, axis=0)
     features = build_features(coords)
     feature_count = features.shape[0]
     inverse_total = 1.0 / (features.shape[1] * lax.axis_size("tm"))

time: 183 us -> 137 us (0.75)
  waiting for transfers between devices: 139 us -> 84.2 us
  blocking collectives: 0 us -> 11.3 us
    psum x1 -> x0, waiting for transfers between devices: 56 us -> none  [on_device(): coords = lax.psum(partial_proj, 'dof')]
    all_gather x0 -> x1, blocking collectives: none -> 11.3 us  [on_device(): blocks = lax.all_gather(partial_proj, 'dof')]
  transfers between devices with their start and end apart: 2 -> 1, of which waited for: 2 -> 1; matrix products, arithmetic and copies ran while one was open for 0% -> 0% of each run, Pallas kernels for 0% -> 0%
where the time goes in v2:
time: 137 us; the launch traced here: 136 us
  waiting for transfers between devices  84.2 us (61%)
  local copies, waits for them, and re-layouts  14.4 us (11%)
  between operations  14.1 us (10%)
  blocking collectives  11.3 us (8%)
  matrix products  8.67 us (6%)
  other arithmetic  3.57 us (3%)
    all_gather x1, waiting for transfers between devices, on_device(): piece = lax.all_gather(features, 'tm', axis=1, tiled=True)  84.2 us
    gather x2, local copies, waits for them, and re-layouts, build_features(): quad = coords[upper_i, :] * coords[upper_j, :]  12.7 us
    all_gather x1, blocking collectives, on_device(): blocks = lax.all_gather(partial_proj, 'dof')  11.3 us
    dot_general x1, matrix products, on_device(): lax.dot_general(basis, snapshots, (((0,), (0,)), ((), ())), preferred_ele...  5.78 us
    dot_general x1, matrix products, on_device(): lax.dot_general(row_part, col_part, (((1,), (1,)), ((), ())), preferred_e...  2.89 us
  transfers between devices with their start and end apart: 1, of which 1 were waited for; matrix products, arithmetic and copies ran while one was open for 0% of the time, Pallas kernels for 0%

profile of v2, /device:TPU:0, one launch (start us, length us, event | category | flops | bytes accessed | tf_op | source)
XLA Modules:
  0.0 136.4 jit_solution(1558212727610732517)
XLA Ops:
  7.2 0.0 copy-start
  7.2 0.0 copy-start.3
  7.2 0.0 all-gather.3.cloned.1.call-start
  7.2 1.7 %copy-done = bf16[20480,64]{0,1:T(8,128)(2,1)S(1)} copy-done((bf16[20480,64]{0,1:T(8,128)(2,1)S(1)}, bf16[20480,64]{0,1:T(8,128)(2,1)}, u32[]{:S(2)}) %copy-start) | copy-done | bytes 2621464
  8.9 5.8 %fusion.3 = f32[64,256]{1,0:T(8,128)S(1)} fusion(bf16[20480,64]{0,1:T(8,128)(2,1)S(1)} %copy-done, bf16[20480,256]{1,0:T(8,128)(2,1)} %param.6), kind=kOutput, calls=%fused_computation.10 | convolution fusion | flops 671088640 | bytes 13172736 | tf_op jit(solution)/shard_map/dot_general | solution.py:16
  14.7 11.3 %all-gather = f32[512,256]{1,0:T(8,128)S(1)} all-gather(f32[64,256]{1,0:T(8,128)S(1)} %fusion.3), channel_id=2, replica_groups=mesh['dof'=8,'tm'=4] {'dof'}, dimensions={0}, use_global_device_ids=true | all-gather | bytes 589824 | tf_op jit(solution)/shard_map/all_gather | solution.py:19
  26.0 0.0 copy-done.3
  26.1 0.0 copy-start.1
  26.1 0.0 copy-start.2
  26.1 6.4 %gather_fusion = f32[2080,256]{1,0:T(8,128)} fusion(f32[64,256]{1,0:T(8,128)S(1)} %reduce_sum.9, s32[3072]{0:T(1024)S(1)} %pad_clamp_fusion.1), kind=kCustom, calls=%fused_computation | custom fusion | bytes 4268160 | tf_op jit(solution)/shard_map/gather | solution.py:11
  32.5 0.0 copy-done.2
  32.5 0.0 copy-done.1
  32.5 6.4 %gather_fusion.1 = f32[2080,256]{1,0:T(8,128)} fusion(f32[64,256]{1,0:T(8,128)S(1)} %reduce_sum.9, s32[3072]{0:T(1024)S(1)} %pad_clamp_fusion), kind=kCustom, calls=%fused_computation.1 | custom fusion | bytes 4268160 | tf_op jit(solution)/shard_map/gather | solution.py:11
  38.9 2.5 %multiply_convert_fusion = bf16[2080,256]{1,0:T(8,128)(2,1)S(1)} fusion(f32[2080,256]{1,0:T(8,128)} %gather_fusion, f32[2080,256]{1,0:T(8,128)} %gather_fusion.1), kind=kLoop, calls=%fused_computation.2 | loop fusion | flops 1064960 | bytes 5324800 | tf_op jit(solution)/shard_map/convert.1
  41.4 1.1 pad_maximum_fusion
  42.4 0.0 all-gather.3.cloned.1.call-update
  42.4 84.2 %all-gather.3.cloned.1.call-done = bf16[2144,1024]{1,0:T(8,128)(2,1)} async-done(((bf16[2144,256]{1,0:T(8,128)(2,1)}), bf16[2144,1024]{1,0:T(8,128)(2,1)}) %all-gather.3.cloned.1.call-update) | async-done | bytes 4390928 | tf_op jit(solution)/shard_map/all_gather | solution.py:29
  126.6 2.9 %convolution_multiply_fusion = f32[536,268]{0,1:T(8,128)} fusion(bf16[2144,1024]{1,0:T(8,128)(2,1)} %all-gather.3.cloned.1.call-done, s32[]{:T(128)S(6)} %select_n.14, s32[]{:T(128)S(6)} %select_n.15), kind=kOutput, calls=%fused_computation.3 | convolution fusion | flops 294334752 | bytes 2229384 | tf_op jit(solution)/shard_map/dot_general | solution.py:32
  (4 shorter events, 0.1 us)
Async XLA Ops:
  7.2 1.7 %copy-start = (bf16[20480,64]{0,1:T(8,128)(2,1)S(1)}, bf16[20480,64]{0,1:T(8,128)(2,1)}, u32[]{:S(2)}) copy-start(bf16[20480,64]{0,1:T(8,128)(2,1)} %param.7) | copy-start | bytes 7864324
  7.2 18.9 %copy-start.3 = (s32[2080]{0:T(1024)S(1)}, s32[2080]{0:T(1024)}, u32[]{:S(2)}) copy-start(s32[2080]{0:T(1024)} %constant.34) | copy-start | bytes 24964
  7.2 119.5 %all-gather.3.cloned.1.call-start = ((), (), s32[]{:S(2)}) async-start(), calls=%async_computation | async-start | bytes 5488640 | tf_op jit(solution)/shard_map/all_gather | solution.py:29
  26.1 6.4 %copy-start.1 = (f32[64,256]{1,0:T(8,128)}, f32[64,256]{1,0:T(8,128)S(1)}, u32[]{:S(2)}) copy-start(f32[64,256]{1,0:T(8,128)S(1)} %reduce_sum.9) | copy-start | bytes 196612
  26.1 6.4 %copy-start.2 = (s32[2080]{0:T(1024)S(1)}, s32[2080]{0:T(1024)}, u32[]{:S(2)}) copy-start(s32[2080]{0:T(1024)} %constant.35) | copy-start | bytes 24964
Sparse Core Ops, SparseCore 0:
  42.6 84.0 all-gather.2
